TPU v7x, 32 devices: a whole 2x2x4 slice. The times are simulated.
32 devices in a mesh: row: 4 (over y, core), col: 8 (over z, x).
Axes of the slice: x: 2, y: 2, z: 4, core: 2. Of those that a mesh axis runs over, the one named last changes fastest.
Arguments:
- lower_inverse: float32 [4, 8, 1024, 1024], P('row', 'col'), may hold values from -1 to 2, as said below
- upper_inverse: float32 [4, 8, 1024, 1024], P('row', 'col'), may hold values from -1 to 2, as said below
- left_coupling: bfloat16 [4, 8, 512, 1024], P('row', 'col'), may hold values from -0.1875 to 0.1875
- right_pieces: float32 [8, 1024, 2048], P('col', None, 'row'), may hold values from -6 to 6
- interface_block: int32 [4, 8, 4], P('row', 'col'), may hold values from 0 to 7, all different within a row
- a_gg: float32 [4, 1024, 2048], P('row', 'col'), may hold values from -6 to 6
- panel_order: int32 [4], replicated, may hold values from 0 to 3, each once
Outputs:
- schur: float32 [4, 1024, 2048], P('row', 'col')
Inputs may be any that keep to these rules, and one draw needn't show every extreme that they name: `interface_block`: the 4 block ids of one subdomain are distinct. `panel_order`: A permutation of the column blocks. `lower_inverse`: lower triangular, diagonal between 1 and 2. `upper_inverse`: upper triangular, diagonal between 1 and 2.
All inputs are finite; a program needn't handle non-finite values.
Results may differ from a plain program's by a relative error of at most 0.0028.
Values sent between devices are 32-bit elements; how exact they have to be, the bound alone decides.
A program may use at most 128 MiB of HBM per device.

v0:
```python
import jax
import jax.numpy as jnp
from jax import lax
from jax.sharding import PartitionSpec as P


def column_order(panel_order):
    length = panel_order.shape[0]
    positions = jnp.arange(length, dtype=jnp.int32)
    hits = (panel_order[:, None] == positions[None, :]).astype(jnp.int32)
    return jnp.sum(hits * positions[:, None], axis=0)


def couple(lower_mat, upper_mat, left_mat, panel):
    halfway = jnp.dot(
        lower_mat, panel, precision=lax.Precision.HIGHEST, preferred_element_type=jnp.float32
    )
    solved = jnp.dot(
        upper_mat, halfway, precision=lax.Precision.HIGHEST, preferred_element_type=jnp.float32
    )
    solved = solved.astype(jnp.bfloat16)
    return jnp.dot(left_mat, solved, preferred_element_type=jnp.float32)


def place_rows(coupled, block_ids, block_total):
    block_count = block_ids.shape[0]
    block_rows = coupled.shape[0] // block_count
    targets = jnp.arange(block_total, dtype=jnp.int32)
    placed = (block_ids[:, None] == targets[None, :]).astype(jnp.float32)
    shaped = coupled.reshape(block_count, block_rows, coupled.shape[1])
    spread = jnp.einsum("kb,kwp->bwp", placed, shaped, precision=lax.Precision.HIGHEST)
    return spread.reshape(block_total * block_rows, coupled.shape[1])


def per_device(
    lower_inverse, upper_inverse, left_coupling, right_pieces, interface_block, a_gg, panel_order
):
    lower_mat = lower_inverse[0, 0]
    upper_mat = upper_inverse[0, 0]
    left_mat = left_coupling[0, 0]
    block_ids = interface_block[0, 0]
    row_count = lax.axis_size("row")
    coupled = couple(
        lower_mat, upper_mat, left_mat, lax.all_gather(right_pieces, "row", axis=2, tiled=True)[0]
    )
    order = column_order(panel_order)
    width_piece = right_pieces.shape[2]
    height = coupled.shape[0]
    coupled = coupled.reshape(height, row_count, width_piece)[:, order, :].reshape(
        height, row_count * width_piece
    )
    block_rows = a_gg.shape[1]
    owned = lax.psum_scatter(
        place_rows(coupled, block_ids, block_rows * lax.axis_size("col") // block_rows),
        "col",
        scatter_dimension=0,
        tiled=True,
    )
    return (a_gg[0] - owned)[None]


def solution(mesh):
    return jax.shard_map(
        per_device,
        mesh=mesh,
        in_specs=(
            P("row", "col", None, None),
            P("row", "col", None, None),
            P("row", "col", None, None),
            P("col", None, "row"),
            P("row", "col", None),
            P("row", "col", None),
            P(),
        ),
        out_specs=P("row", "col", None),
        check_vma=False,
    )
```

profile of v0, /device:TPU:0, one launch (start us, length us, event | category | flops | bytes accessed | tf_op | source)
XLA Modules:
  0.0 355.0 jit_solution(11095625044394549900)
XLA Ops:
  6.5 0.0 copy-start
  6.5 0.0 all-gather.2.cloned.1.call-start
  6.5 0.7 all-gather.2.cloned.1.call-update
  7.3 0.0 reduce-scatter.2.cloned.1.call-start
  7.3 0.7 select_reduce_fusion
  8.1 61.9 %all-gather.2.cloned.1.call-done = f32[1,1024,2048]{2,1,0:T(8,128)} async-done(((f32[1,1024,512]{2,1,0:T(8,128)}), f32[1,1024,2048]{2,1,0:T(8,128)}) %all-gather.2.cloned.1.call-update) | async-done | bytes 8388624 | tf_op jit(solution)/shard_map/all_gather | solution.py:44
  69.9 0.0 copy-start.4
  69.9 29.7 %fusion = f32[1024,2048]{1,0:T(8,128)S(1)} fusion(f32[1,1024,2048]{2,1,0:T(8,128)} %all-gather.2.cloned.1.call-done, f32[1,1,1024,1024]{3,2,1,0:T(8,128)} %param.7), kind=kOutput, calls=%fused_computation.1 | convolution fusion | flops 25769803776 | bytes 20971520 | tf_op jit(solution)/shard_map/dot_general | solution.py:15
  99.7 0.0 copy-done.4
  99.7 53.0 %fusion.2 = bf16[2048,1024]{1,0:T(8,128)(2,1)S(1)} fusion(f32[1024,2048]{1,0:T(8,128)S(1)} %fusion, f32[1,1,1024,1024]{3,2,1,0:T(8,128)S(1)} %copy-done.4), kind=kOutput, calls=%fused_computation.3 | convolution fusion | flops 25769803776 | bytes 16777216 | tf_op jit(solution)/shard_map/dot_general | solution.py:18
  152.7 0.0 copy-done
  152.7 4.4 %fusion.7 = f32[2048,512]{1,0:T(8,128)} fusion(bf16[2048,1024]{1,0:T(8,128)(2,1)S(1)} %fusion.2, bf16[1,1,512,1024]{3,2,1,0:T(8,128)(2,1)S(1)} %copy-done), kind=kOutput, calls=%fused_computation.8 | convolution fusion | flops 2147483648 | bytes 9437184 | tf_op jit(solution)/shard_map/dot_general | solution.py:22
  157.0 5.2 %copy.14 = f32[512,4,512]{2,0,1:T(8,128)} copy(f32[512,4,512]{0,2,1:T(8,128)} %bitcast.35) | data formatting | bytes 8388608 | tf_op jit(solution)/shard_map/reshape | solution.py:49
  162.3 5.0 %gather_fusion = f32[4,512,512]{2,1,0:T(8,128)} fusion(f32[512,4,512]{2,0,1:T(8,128)} %copy.14, s32[1024]{0:T(1024)S(1)} %pad_clamp_fusion), kind=kCustom, calls=%fused_computation | custom fusion | bytes 8388624 | tf_op jit(solution)/shard_map/gather | solution.py:49
  167.3 6.8 %copy.15 = f32[512,4,512]{2,1,0:T(4,128)} copy(f32[512,4,512]{2,0,1:T(8,128)} %bitcast.34) | data formatting | bytes 8388608 | tf_op jit(solution)/shard_map/gather | solution.py:49
  174.1 0.0 copy-start.3
  174.1 6.1 %reshape_reshape.3 = f32[4,128,2048]{2,1,0:T(8,128)} reshape(f32[512,4,512]{2,1,0:T(4,128)} %copy.15) | data formatting | bytes 8388608 | tf_op jit(solution)/shard_map/reshape;reshape | solution.py:30
  180.2 0.0 copy-done.3
  180.2 9.9 %fusion.5 = f32[8,128,2048]{2,0,1:T(8,128)S(1)} fusion(f32[4,128,2048]{2,1,0:T(8,128)} %reshape_reshape.3, s32[4]{0:T(128)S(1)} %bitcast.36), kind=kOutput, calls=%fused_computation.6 | convolution fusion | flops 100663328 | bytes 12582928 | tf_op jit(solution)/shard_map/kb,kwp->bwp/dot_general | solution.py:31
  190.1 8.1 %copy.17 = f32[8,128,2048]{2,1,0:T(8,128)} copy(f32[8,128,2048]{2,0,1:T(8,128)S(1)} %fusion.5) | data formatting | bytes 16777216 | tf_op jit(solution)/shard_map/kb,kwp->bwp/dot_general | solution.py:31
  198.2 0.0 copy-start.1
  198.2 0.0 copy-start.2
  198.2 0.0 reduce-scatter.2.cloned.1.call-update
  198.2 147.6 %reduce-scatter.2.cloned.1.call-done = f32[128,2048]{1,0:T(8,128)} async-done(((f32[1024,2048]{1,0:T(8,128)}), f32[128,2048]{1,0:T(8,128)}) %reduce-scatter.2.cloned.1.call-update) | async-done | bytes 1048592 | tf_op jit(solution)/shard_map/reduce_scatter | solution.py:53
  345.8 0.0 copy-done.2
  345.8 2.3 fusion.10
  348.1 0.0 copy-done.1
  (2 shorter events, 0.0 us)
Async XLA Ops:
  6.5 146.1 %copy-start = (bf16[1,1,512,1024]{3,2,1,0:T(8,128)(2,1)S(1)}, bf16[1,1,512,1024]{3,2,1,0:T(8,128)(2,1)}, u32[]{:S(2)}) copy-start(bf16[1,1,512,1024]{3,2,1,0:T(8,128)(2,1)} %param.9) | copy-start | bytes 3145732
  6.5 63.4 %all-gather.2.cloned.1.call-start = ((), (), s32[]{:S(2)}) async-start(), calls=%async_computation.1 | async-start | bytes 10485760 | tf_op jit(solution)/shard_map/all_gather | solution.py:44
  7.3 338.5 %reduce-scatter.2.cloned.1.call-start = ((), (), s32[]{:S(2)}) async-start(), calls=%async_computation.2 | async-start | bytes 9437184 | tf_op jit(solution)/shard_map/reduce_scatter | solution.py:53
  69.9 29.8 %copy-start.4 = (f32[1,1,1024,1024]{3,2,1,0:T(8,128)S(1)}, f32[1,1,1024,1024]{3,2,1,0:T(8,128)}, u32[]{:S(2)}) copy-start(f32[1,1,1024,1024]{3,2,1,0:T(8,128)} %param.8) | copy-start | bytes 12582916
  174.1 6.1 %copy-start.3 = (s32[1,1,4]{2,1,0:T(1,128)S(1)}, s32[1,1,4]{2,1,0:T(1,128)}, u32[]{:S(2)}) copy-start(s32[1,1,4]{2,1,0:T(1,128)} %param.11) | copy-start | bytes 52
  198.2 149.9 %copy-start.1 = (bf16[1,1,512,1024]{3,2,1,0:T(8,128)(2,1)S(1)}, bf16[1,1,512,1024]{3,2,1,0:T(8,128)(2,1)}, u32[]{:S(2)}) copy-start(bf16[1,1,512,1024]{3,2,1,0:T(8,128)(2,1)} %param.9) | copy-start | bytes 3145732
  198.2 147.6 %copy-start.2 = (f32[1,128,2048]{2,1,0:T(8,128)S(1)}, f32[1,128,2048]{2,1,0:T(8,128)}, u32[]{:S(2)}) copy-start(f32[1,128,2048]{2,1,0:T(8,128)} %param.12) | copy-start | bytes 3145732
Sparse Core Ops, SparseCore 0:
  8.9 60.9 all-gather.1
  198.3 147.4 reduce-scatter.1
where the time goes:
time: 355 us
  waiting for transfers between devices  210 us (59%)
  matrix products  97 us (27%)
  local copies, waits for them, and re-layouts  31.2 us (9%)
  between operations  13.4 us (4%)
    reduce_scatter x1, waiting for transfers between devices, per_device(): lax.psum_scatter(place_rows(coupled, block_ids, block_rows * lax.axis_siz...  148 us
    all_gather x1, waiting for transfers between devices, per_device(): lax.all_gather(right_pieces, 'row', axis=2, tiled=True)[0]  61.9 us
    dot_general x1, matrix products, couple(): jnp.dot(upper_mat, halfway, precision=lax.Precision.HIGHEST, preferred_el...  53 us
    dot_general x1, matrix products, couple(): jnp.dot(lower_mat, panel, precision=lax.Precision.HIGHEST, preferred_elem...  29.7 us
    gather x2, local copies, waits for them, and re-layouts, per_device(): coupled.reshape(height, row_count, width_piece)[:, order, :]  11.8 us
    dot_general x1, matrix products, place_rows(): jnp.einsum('kb,kwp->bwp', placed, shaped, precision=lax.Precision.HIGHEST)  9.92 us
    dot_general x1, local copies, waits for them, and re-layouts, place_rows(): jnp.einsum('kb,kwp->bwp', placed, shaped, precision=lax.Precision.HIGHEST)  8.08 us
  transfers between devices with their start and end apart: 2, of which 2 were waited for; matrix products, arithmetic and copies ran while one was open for 0% of the time, Pallas kernels for 0%

commit v1 on v0

--- a/solution.py
+++ b/solution.py
@@ -41,7 +41,10 @@
     block_ids = interface_block[0, 0]
     row_count = lax.axis_size("row")
     coupled = couple(
-        lower_mat, upper_mat, left_mat, lax.all_gather(right_pieces, "row", axis=2, tiled=True)[0]
+        lower_mat,
+        upper_mat,
+        left_mat,
+        jnp.concatenate(lax.all_gather(right_pieces, "row"), axis=2)[0],
     )
     order = column_order(panel_order)
     width_piece = right_pieces.shape[2]

time: 355 us -> 370 us (1.042); the launches traced: 355 us -> 364 us
  local copies, waits for them, and re-layouts: 31.2 us -> 39.9 us
    all_gather x0 -> x1, local copies, waits for them, and re-layouts: none -> 8.73 us  [per_device(): lax.all_gather(right_pieces, 'row')]
where the time goes in v1:
time: 370 us; the launch traced here: 364 us
  waiting for transfers between devices  210 us (57%)
  matrix products  97.3 us (26%)
  local copies, waits for them, and re-layouts  39.9 us (11%)
  between operations  13.7 us (4%)
    reduce_scatter x1, waiting for transfers between devices, per_device(): lax.psum_scatter(place_rows(coupled, block_ids, block_rows * lax.axis_siz...  148 us
    all_gather x1, waiting for transfers between devices, per_device(): lax.all_gather(right_pieces, 'row')  61.9 us
    dot_general x1, matrix products, couple(): jnp.dot(upper_mat, halfway, precision=lax.Precision.HIGHEST, preferred_el...  53.2 us
    dot_general x1, matrix products, couple(): jnp.dot(lower_mat, panel, precision=lax.Precision.HIGHEST, preferred_elem...  29.8 us
    gather x2, local copies, waits for them, and re-layouts, per_device(): coupled.reshape(height, row_count, width_piece)[:, order, :]  11.8 us
    dot_general x1, matrix products, place_rows(): jnp.einsum('kb,kwp->bwp', placed, shaped, precision=lax.Precision.HIGHEST)  9.86 us
    all_gather x1, local copies, waits for them, and re-layouts, per_device(): lax.all_gather(right_pieces, 'row')  8.73 us
    dot_general x1, local copies, waits for them, and re-layouts, place_rows(): jnp.einsum('kb,kwp->bwp', placed, shaped, precision=lax.Precision.HIGHEST)  8.08 us
  transfers between devices with their start and end apart: 2, of which 2 were waited for; matrix products, arithmetic and copies ran while one was open for 0% of the time, Pallas kernels for 0%

profile of v1, /device:TPU:0, one launch (start us, length us, event | category | flops | bytes accessed | tf_op | source)
XLA Modules:
  0.0 364.2 jit_solution(5811372967575138404)
XLA Ops:
  6.5 0.0 copy-start
  6.5 0.0 all-gather.3.cloned.1.call-start
  6.5 0.7 all-gather.3.cloned.1.call-update
  7.3 0.0 reduce-scatter.2.cloned.1.call-start
  7.3 0.7 select_reduce_fusion
  8.1 61.9 %all-gather.3.cloned.1.call-done = f32[4,1024,512]{2,1,0:T(8,128)} async-done(((f32[1,1024,512]{2,1,0:T(8,128)}), f32[4,1024,512]{2,1,0:T(8,128)}) %all-gather.3.cloned.1.call-update) | async-done | bytes 8388624 | tf_op jit(solution)/shard_map/all_gather | solution.py:47
  69.9 8.7 %copy.21 = f32[4,1024,512]{1,2,0:T(8,128)} copy(f32[4,1024,512]{2,1,0:T(8,128)} %all-gather.3.cloned.1.call-done) | data formatting | bytes 16777216 | tf_op jit(solution)/shard_map/all_gather | solution.py:47
  78.6 0.0 copy-start.4
  78.6 29.8 %fusion.2 = f32[1024,2048]{1,0:T(8,128)S(1)} fusion(f32[1024,2048]{0,1:T(8,128)} %bitcast.38, f32[1,1,1024,1024]{3,2,1,0:T(8,128)} %param.7), kind=kOutput, calls=%fused_computation.3 | convolution fusion | flops 25769803776 | bytes 20971520 | tf_op jit(solution)/shard_map/dot_general | solution.py:15
  108.5 0.0 copy-done.4
  108.5 53.2 %fusion = bf16[2048,1024]{1,0:T(8,128)(2,1)S(1)} fusion(f32[1024,2048]{1,0:T(8,128)S(1)} %fusion.2, f32[1,1,1024,1024]{3,2,1,0:T(8,128)S(1)} %copy-done.4), kind=kOutput, calls=%fused_computation.1 | convolution fusion | flops 25769803776 | bytes 16777216 | tf_op jit(solution)/shard_map/dot_general | solution.py:18
  161.7 0.0 copy-done
  161.7 4.4 %fusion.6 = f32[2048,512]{1,0:T(8,128)} fusion(bf16[2048,1024]{1,0:T(8,128)(2,1)S(1)} %fusion, bf16[1,1,512,1024]{3,2,1,0:T(8,128)(2,1)S(1)} %copy-done), kind=kOutput, calls=%fused_computation.7 | convolution fusion | flops 2147483648 | bytes 9437184 | tf_op jit(solution)/shard_map/dot_general | solution.py:22
  166.1 5.2 %copy.22 = f32[512,4,512]{2,0,1:T(8,128)} copy(f32[512,4,512]{0,2,1:T(8,128)} %bitcast.39) | data formatting | bytes 8388608 | tf_op jit(solution)/shard_map/reshape | solution.py:52
  171.3 5.0 %gather_fusion = f32[4,512,512]{2,1,0:T(8,128)} fusion(f32[512,4,512]{2,0,1:T(8,128)} %copy.22, s32[1024]{0:T(1024)S(1)} %pad_clamp_fusion), kind=kCustom, calls=%fused_computation | custom fusion | bytes 8388624 | tf_op jit(solution)/shard_map/gather | solution.py:52
  176.3 6.8 %copy.23 = f32[512,4,512]{2,1,0:T(4,128)} copy(f32[512,4,512]{2,0,1:T(8,128)} %bitcast.37) | data formatting | bytes 8388608 | tf_op jit(solution)/shard_map/gather | solution.py:52
  183.1 0.0 copy-start.3
  183.1 6.1 %reshape_reshape.3 = f32[4,128,2048]{2,1,0:T(8,128)} reshape(f32[512,4,512]{2,1,0:T(4,128)} %copy.23) | data formatting | bytes 8388608 | tf_op jit(solution)/shard_map/reshape;reshape | solution.py:30
  189.2 0.0 copy-done.3
  189.2 9.9 %fusion.4 = f32[8,128,2048]{2,0,1:T(8,128)S(1)} fusion(f32[4,128,2048]{2,1,0:T(8,128)} %reshape_reshape.3, s32[4]{0:T(128)S(1)} %bitcast.40), kind=kOutput, calls=%fused_computation.5 | convolution fusion | flops 100663328 | bytes 12582928 | tf_op jit(solution)/shard_map/kb,kwp->bwp/dot_general | solution.py:31
  199.1 8.1 %copy.25 = f32[8,128,2048]{2,1,0:T(8,128)} copy(f32[8,128,2048]{2,0,1:T(8,128)S(1)} %fusion.4) | data formatting | bytes 16777216 | tf_op jit(solution)/shard_map/kb,kwp->bwp/dot_general | solution.py:31
  207.2 0.0 copy-start.1
  207.2 0.0 copy-start.2
  207.2 0.0 reduce-scatter.2.cloned.1.call-update
  207.2 147.6 %reduce-scatter.2.cloned.1.call-done = f32[128,2048]{1,0:T(8,128)} async-done(((f32[1024,2048]{1,0:T(8,128)}), f32[128,2048]{1,0:T(8,128)}) %reduce-scatter.2.cloned.1.call-update) | async-done | bytes 1048592 | tf_op jit(solution)/shard_map/reduce_scatter | solution.py:56
  354.8 0.0 copy-done.2
  354.8 2.3 fusion.9
  357.1 0.0 copy-done.1
  (2 shorter events, 0.0 us)
Async XLA Ops:
  6.5 155.2 %copy-start = (bf16[1,1,512,1024]{3,2,1,0:T(8,128)(2,1)S(1)}, bf16[1,1,512,1024]{3,2,1,0:T(8,128)(2,1)}, u32[]{:S(2)}) copy-start(bf16[1,1,512,1024]{3,2,1,0:T(8,128)(2,1)} %param.9) | copy-start | bytes 3145732
  6.5 63.4 %all-gather.3.cloned.1.call-start = ((), (), s32[]{:S(2)}) async-start(), calls=%async_computation.2 | async-start | bytes 10485760 | tf_op jit(solution)/shard_map/all_gather | solution.py:47
  7.3 347.5 %reduce-scatter.2.cloned.1.call-start = ((), (), s32[]{:S(2)}) async-start(), calls=%async_computation.1 | async-start | bytes 9437184 | tf_op jit(solution)/shard_map/reduce_scatter | solution.py:56
  78.6 29.8 %copy-start.4 = (f32[1,1,1024,1024]{3,2,1,0:T(8,128)S(1)}, f32[1,1,1024,1024]{3,2,1,0:T(8,128)}, u32[]{:S(2)}) copy-start(f32[1,1,1024,1024]{3,2,1,0:T(8,128)} %param.8) | copy-start | bytes 12582916
  183.1 6.1 %copy-start.3 = (s32[1,1,4]{2,1,0:T(1,128)S(1)}, s32[1,1,4]{2,1,0:T(1,128)}, u32[]{:S(2)}) copy-start(s32[1,1,4]{2,1,0:T(1,128)} %param.11) | copy-start | bytes 52
  207.2 149.9 %copy-start.1 = (bf16[1,1,512,1024]{3,2,1,0:T(8,128)(2,1)S(1)}, bf16[1,1,512,1024]{3,2,1,0:T(8,128)(2,1)}, u32[]{:S(2)}) copy-start(bf16[1,1,512,1024]{3,2,1,0:T(8,128)(2,1)} %param.9) | copy-start | bytes 3145732
  207.2 147.6 %copy-start.2 = (f32[1,128,2048]{2,1,0:T(8,128)S(1)}, f32[1,128,2048]{2,1,0:T(8,128)}, u32[]{:S(2)}) copy-start(f32[1,128,2048]{2,1,0:T(8,128)} %param.12) | copy-start | bytes 3145732
Sparse Core Ops, SparseCore 0:
  8.9 60.9 all-gather.2
  207.3 147.4 reduce-scatter.1
